TPU v7x, 32 devices: a whole 2x2x4 slice. The times are simulated.
32 devices in a mesh: gx: 8 (over y, x, core), gy: 4 (over z).
Axes of the slice: x: 2, y: 2, z: 4, core: 2. Of those that a mesh axis runs over, the one named last changes fastest.
Arguments:
- volts: float32 [32, 4, 64, 512], P(None, None, 'gx', 'gy'), may hold values from -6 to 6
- cap: float32 [4, 64, 512], P(None, 'gx', 'gy'), may hold values from 0.05 to 1
- cond_x: float32 [4, 64, 512], P(None, 'gx', 'gy'), may hold values from 0.5 to 2
- cond_y: float32 [4, 64, 512], P(None, 'gx', 'gy'), may hold values from 0.5 to 2
- via: float32 [4, 64, 512], P(None, 'gx', 'gy'), may hold values from 0.2 to 2
- waveforms: float32 [64, 64], replicated, may hold values from -6 to 6
- placement: int32 [262144, 1], P(('gx', 'gy')), may hold values from 0 to 31; in each aligned block of 8192 rows (0 to 8191, 8192 to 16383, ...) at most 512 rows name the same one
- cells: int32 [262144], P(('gx', 'gy')), may hold values from 0 to 1023
- wave_ids: int32 [262144], P(('gx', 'gy')), may hold values from 0 to 63
- amps: float32 [262144], P(('gx', 'gy')), may hold values from 0.5 to 4
Outputs:
- volts_out: float32 [32, 4, 64, 512], P(None, None, 'gx', 'gy')
- residual: float32 [32, 4, 64, 512], P(None, None, 'gx', 'gy')
Inputs may be any that keep to these rules, and one draw needn't show every extreme that they name: `placement`: in each device's block of 8192 rows no tile is named more than 512 times, a bound that some block reaches.
All inputs are finite; a program needn't handle non-finite values.
Results may differ from a plain program's by a relative error of at most 0.0029.
Values may be sent and summed in bfloat16 or wider, within the bound.
A program may use at most 64 MiB of HBM per device.

v0:
```python
import jax
import jax.numpy as jnp
from jax import lax
from jax.sharding import PartitionSpec as P

ITERS = 3


def with_halo(block, sides, width):
    for axis, dim in sides:
        count = lax.axis_size(axis)
        forward = [(i, i + 1) for i in range(count - 1)]
        backward = [(target, source) for source, target in forward]
        low = lax.ppermute(
            lax.slice_in_dim(block, block.shape[dim] - width, None, axis=dim), axis, forward
        )
        high = lax.ppermute(lax.slice_in_dim(block, 0, width, axis=dim), axis, backward)
        block = jnp.concatenate([low, block, high], axis=dim)
    return block


def shifted(x, axis, by):
    length = lax.axis_size(axis)
    pairs = [(i, i + by) for i in range(length) if 0 <= i + by < length]
    return lax.ppermute(x, axis, pairs)


def gram(left, right):
    left_rows = left.reshape(left.shape[0], -1)
    right_rows = right.reshape(right.shape[0], -1)
    return lax.dot_general(
        left_rows, right_rows, (((1,), (1,)), ((), ())), precision=lax.Precision.HIGHEST
    )


def combine(coef, field):
    return jnp.einsum("st,slxy->tlxy", coef, field, precision=lax.Precision.HIGHEST)


def spd_solve(matrix, right):
    factor = jnp.linalg.cholesky(matrix)
    return jax.scipy.linalg.cho_solve((factor, True), right)


def make_currents(waveforms, kinds, scales):
    table_hits = (
        jnp.arange(waveforms.shape[1], dtype=jnp.int32)[:, None] == kinds[None, :]
    ).astype(jnp.float32)
    picked = jnp.dot(waveforms, table_hits, precision=lax.Precision.HIGHEST)
    return (picked * scales[None, :]).astype(jnp.bfloat16)


def operate(field, cap, cond_x, cond_x_low, cond_y, cond_y_low, via, via_low):
    padded = with_halo(field, (("gx", 2), ("gy", 3)), 1)
    zero_layer = jnp.zeros_like(field[:, :1])
    upper = jnp.concatenate([field[:, 1:], zero_layer], axis=1)
    lower = jnp.concatenate([zero_layer, field[:, :-1]], axis=1)
    result = cap * field
    result = result + cond_x * (field - padded[:, :, 2:, 1:-1])
    result = result + cond_x_low * (field - padded[:, :, :-2, 1:-1])
    result = result + cond_y * (field - padded[:, :, 1:-1, 2:])
    result = result + cond_y_low * (field - padded[:, :, 1:-1, :-2])
    result = result + via * (field - upper) + via_low * (field - lower)
    return result


def body(volts, cap, cond_x, cond_y, via, waveforms, placement, cells, wave_ids, amps):
    devices = lax.axis_size(("gx", "gy"))
    scenarios = volts.shape[0]
    steps = waveforms.shape[0] // scenarios
    tile_x = volts.shape[2]
    tile_y = volts.shape[3]
    die_cells = tile_x * tile_y
    slots_all = 2 * cells.shape[0]
    capacity = slots_all // devices
    target = placement[:, 0]
    target_hits = (jnp.arange(devices, dtype=jnp.int32)[:, None] == target[None, :]).astype(
        jnp.int32
    )
    running = jnp.cumsum(target_hits, axis=1) - 1
    position = jnp.sum(target_hits * running, axis=0)
    slot_index = target * capacity + position
    currents = make_currents(waveforms, wave_ids, amps)
    packed = jnp.zeros((currents.shape[0], slots_all), jnp.bfloat16).at[:, slot_index].set(currents)
    cell_slots = jnp.zeros((1, slots_all), jnp.int32).at[0, slot_index].set(cells)
    arrived, cell_slots = (
        lax.all_to_all(packed, ("gx", "gy"), split_axis=1, concat_axis=1, tiled=True),
        lax.all_to_all(cell_slots, ("gx", "gy"), split_axis=1, concat_axis=1, tiled=True),
    )
    block_rows = min(1024, slots_all)
    block_count = slots_all // block_rows
    cell_line = jnp.arange(die_cells, dtype=jnp.int32)

    def add_block(turn, total):
        piece_values = lax.dynamic_slice_in_dim(arrived, turn * block_rows, block_rows, 1)
        piece_cells = lax.dynamic_slice_in_dim(cell_slots[0], turn * block_rows, block_rows, 0)
        one_hot = (piece_cells[:, None] == cell_line[None, :]).astype(jnp.bfloat16)
        return total + jnp.dot(piece_values, one_hot, preferred_element_type=jnp.float32)

    injected = lax.fori_loop(
        0, block_count, add_block, jnp.zeros((arrived.shape[0], die_cells), jnp.float32)
    )
    injected = injected.reshape(steps, scenarios, tile_x, tile_y)
    rim_x = shifted(cond_x[:, -1:, :], "gx", 1)
    rim_y = shifted(cond_y[:, :, -1:], "gy", 1)
    cond_x_low = jnp.concatenate([rim_x, cond_x[:, :-1, :]], axis=1)
    cond_y_low = jnp.concatenate([rim_y, cond_y[:, :, :-1]], axis=2)
    via_low = jnp.concatenate([jnp.zeros_like(via[:1]), via[:-1]], axis=0)

    def apply_grid(field):
        return operate(field, cap, cond_x, cond_x_low, cond_y, cond_y_low, via, via_low)

    voltage = volts
    residual = volts
    for step in range(steps):
        rhs = cap * voltage
        rhs = rhs.at[:, 0].add(-injected[step])
        iterate = voltage
        residual = rhs - apply_grid(iterate)
        direction = residual
        norm_gram = lax.psum(gram(residual, residual), ("gx", "gy"))
        for sweep in range(ITERS):
            image = apply_grid(direction)
            curve_gram, cross_gram, image_gram = lax.psum(
                (gram(direction, image), gram(residual, image), gram(image, image)), ("gx", "gy")
            )
            step_coef = spd_solve(curve_gram, norm_gram)
            iterate = iterate + combine(step_coef, direction)
            residual = residual - combine(step_coef, image)
            if sweep + 1 < ITERS:
                cross_term = jnp.dot(cross_gram, step_coef, precision=lax.Precision.HIGHEST)
                square_term = jnp.dot(
                    step_coef.T,
                    jnp.dot(image_gram, step_coef, precision=lax.Precision.HIGHEST),
                    precision=lax.Precision.HIGHEST,
                )
                new_gram = norm_gram - cross_term - cross_term.T + square_term
                turn_coef = spd_solve(norm_gram, new_gram)
                direction = residual + combine(turn_coef, direction)
                norm_gram = new_gram
        voltage = iterate
    return (voltage, residual)


def solution(mesh):
    return jax.shard_map(
        body,
        mesh=mesh,
        in_specs=(
            P(None, None, "gx", "gy"),
            P(None, "gx", "gy"),
            P(None, "gx", "gy"),
            P(None, "gx", "gy"),
            P(None, "gx", "gy"),
            P(),
            P(("gx", "gy"), None),
            P(("gx", "gy")),
            P(("gx", "gy")),
            P(("gx", "gy")),
        ),
        out_specs=(P(None, None, "gx", "gy"), P(None, None, "gx", "gy")),
        check_vma=False,
    )
```

profile of v0, /device:TPU:0, one launch (start us, length us, event | category | flops | bytes accessed | tf_op | source)
XLA Modules:
  0.0 647.4 jit_solution(1546838298687216187)
XLA Ops:
  1.6 9.5 %reduce-window.6 = s32[32,64,128]{2,1,0:T(8,128)S(1)} reduce-window(s32[32,64,128]{2,1,0:T(8,128)S(1)} %fusion.11, s32[]{:T(128)} %constant.128.clone.1), window={size=1x1x128 pad=0_0x0_0x127_0}, to_apply=%region_0.0 | reduce-window | flops 33292288 | bytes 2097156 | tf_op jit(solution)/shard_map/reduce-window
  14.9 23.7 %scatter_custom_fusion = bf16[64,16384]{0,1:T(8,128)(2,1)} fusion(s32[8192]{0:T(1024)S(1)} %bitcast.343, bf16[8192,64]{1,0:T(8,128)(2,1)S(1)} %copy.219, bf16[]{:T(256)} %constant.130.clone.1), kind=kCustom, calls=%fused_computation.13 | custom fusion | bytes 2097154 | tf_op jit(solution)/shard_map/scatter | solution.py:84
  38.6 4.8 copy.220
  43.3 7.3 %all-to-all-start = ((bf16[64,32,512]{2,0,1:T(8,128)(2,1)}), bf16[64,32,512]{2,0,1:T(8,128)(2,1)S(1)}, u32[]{:S(2)}, u32[]{:S(2)}) async-start(bf16[64,32,512]{2,0,1:T(8,128)(2,1)} %copy.220), calls=%async_computation | async-start | bytes 4194304 | tf_op jit(solution)/shard_map/all_to_all | solution.py:87
  55.2 3.5 collective-permute-start.4
  58.8 3.7 collective-permute-start.1
  62.9 31.2 %scatter_custom_fusion.1 = s32[16384]{0:T(1024)} fusion(s32[8192]{0:T(1024)S(1)} %broadcast_select_fusion, s32[8192]{0:T(1024)} %param.26, s32[]{:T(128)} %constant.128.clone.1), kind=kCustom, calls=%fused_computation.270 | custom fusion | bytes 66048
  97.6 7.3 %all-to-all-start.1 = ((s32[1,32,512]{2,0,1:T(1,128)}), s32[1,32,512]{2,0,1:T(1,128)}, u32[]{:S(2)}, u32[]{:S(2)}) async-start(s32[1,32,512]{2,0,1:T(1,128)} %bitcast.344), calls=%async_computation.1 | async-start | bytes 131072 | tf_op jit(solution)/shard_map/all_to_all | solution.py:88
  110.3 4.7 collective-permute-start.5
  119.0 53.7 %while.16 = (s32[]{:T(128)}, f32[64,1024]{1,0:T(8,128)}, bf16[64,16384]{1,0:T(8,128)(2,1)}, s32[1,16384]{1,0:T(1,128)}, s32[]{:T(128)}, /*index=5*/s32[]{:T(128)}, s32[]{:T(128)}, s32[]{:T(128)}) while((s32[]{:T(128)}, f32[64,1024]{1,0:T(8,128)}, bf16[64,16384]{1,0:T(8,128)(2,1)}, s32[1,16384]{1,0:T(1,128)}, s32[]{:T(128)}, ...), condition=%wide.region_6.7_spmd.clone, body=%wide.region_5.6_spmd.clone.sunk | while | flops 135397376 | bytes 667797 | solution.py:100
  123.1 2.7 fusion.346
  136.5 2.7 fusion.346
  149.9 2.7 fusion.346
  153.3 2.7 fusion.346
  163.3 2.7 fusion.346
  166.7 2.7 fusion.346
  177.6 3.0 collective-permute-start.7
  183.8 4.8 collective-permute-start.9
  192.3 44.5 %all-reduce.21 = (f32[32,32]{0,1:T(8,128)S(1)}, f32[32,32]{0,1:T(8,128)S(1)}, f32[32,32]{1,0:T(8,128)S(1)}) all-reduce(f32[32,32]{0,1:T(8,128)S(1)} %convolution_bitcast_fusion.18, f32[32,32]{0,1:T(8,128)S(1)} %convolution_bitcast_fusion.19, f32[32,32]{1,0:T(8,128)S(1)} %convolution_bitcast_fusion.17), channel_id=1, replica_groups=mesh['gx'=8,'gy'=4] {'gx','gy'}, use_global_device_ids=true, to_apply=%region_10.12 | all-reduce | flops 3072 | bytes 24576 | tf_op jit(solution)/shard_map/psum | solution.py:121
  236.9 2.9 cholesky.164
  245.4 2.9 cholesky.175
  255.0 2.9 cholesky.197
  259.2 3.0 collective-permute-start.11
  266.5 4.8 collective-permute-start.13
  271.9 3.1 custom-call.20
  279.1 43.3 %all-reduce.20 = (f32[32,32]{0,1:T(8,128)S(1)}, f32[32,32]{1,0:T(8,128)S(1)}, f32[32,32]{1,0:T(8,128)S(1)}) all-reduce(f32[32,32]{0,1:T(8,128)S(1)} %convolution_bitcast_fusion.15, f32[32,32]{1,0:T(8,128)S(1)} %convolution_bitcast_fusion.13, f32[32,32]{1,0:T(8,128)S(1)} %convolution_bitcast_fusion.14), channel_id=1, replica_groups=mesh['gx'=8,'gy'=4] {'gx','gy'}, use_global_device_ids=true, to_apply=%region_12.15 | all-reduce | flops 3072 | bytes 24576 | tf_op jit(solution)/shard_map/psum | solution.py:124
  322.6 2.9 cholesky.186
  333.2 3.0 collective-permute-start.15
  340.4 4.5 collective-permute-start.17
  347.8 43.9 %psum.110 = f32[32,32]{0,1:T(8,128)S(1)} all-reduce(f32[32,32]{0,1:T(8,128)S(1)} %convolution_bitcast_fusion.11), channel_id=1, replica_groups=mesh['gx'=8,'gy'=4] {'gx','gy'}, use_global_device_ids=true, to_apply=%region_15.18 | all-reduce | flops 1024 | bytes 8192 | tf_op jit(solution)/shard_map/psum | solution.py:124
  391.7 2.9 cholesky.208
  400.8 3.0 collective-permute-start.19
  408.1 5.0 collective-permute-start.21
  417.5 3.3 collective-permute-start.23
  425.1 4.6 collective-permute-start.25
  434.3 46.8 %all-reduce.19 = (f32[32,32]{0,1:T(8,128)S(1)}, f32[32,32]{0,1:T(8,128)S(1)}, f32[32,32]{1,0:T(8,128)S(1)}) all-reduce(f32[32,32]{0,1:T(8,128)S(1)} %convolution_bitcast_fusion.8, f32[32,32]{0,1:T(8,128)S(1)} %convolution_bitcast_fusion.9, f32[32,32]{1,0:T(8,128)S(1)} %convolution_bitcast_fusion.7), channel_id=1, replica_groups=mesh['gx'=8,'gy'=4] {'gx','gy'}, use_global_device_ids=true, to_apply=%region_17.20 | all-reduce | flops 3072 | bytes 24576 | tf_op jit(solution)/shard_map/psum | solution.py:121
  481.2 2.9 cholesky.219
  489.7 2.9 cholesky.230
  499.9 2.9 cholesky.252
  504.1 3.0 collective-permute-start.27
  510.3 4.7 collective-permute-start.29
  515.7 3.1 custom-call.25
  522.7 42.7 %all-reduce.18 = (f32[32,32]{0,1:T(8,128)S(1)}, f32[32,32]{1,0:T(8,128)S(1)}, f32[32,32]{1,0:T(8,128)S(1)}) all-reduce(f32[32,32]{0,1:T(8,128)S(1)} %convolution_bitcast_fusion.5, f32[32,32]{1,0:T(8,128)S(1)} %convolution_bitcast_fusion.3, f32[32,32]{1,0:T(8,128)S(1)} %convolution_bitcast_fusion.4), channel_id=1, replica_groups=mesh['gx'=8,'gy'=4] {'gx','gy'}, use_global_device_ids=true, to_apply=%region_19.22 | all-reduce | flops 3072 | bytes 24576 | tf_op jit(solution)/shard_map/psum | solution.py:124
  565.5 2.9 cholesky.241
  576.2 3.0 collective-permute-start.31
  583.3 4.5 collective-permute-start.33
  592.0 44.5 %psum.117 = f32[32,32]{0,1:T(8,128)S(1)} all-reduce(f32[32,32]{0,1:T(8,128)S(1)} %convolution_bitcast_fusion.1), channel_id=1, replica_groups=mesh['gx'=8,'gy'=4] {'gx','gy'}, use_global_device_ids=true, to_apply=%region_22.25 | all-reduce | flops 1024 | bytes 8192 | tf_op jit(solution)/shard_map/psum | solution.py:124
  636.6 2.9 cholesky.263
  (373 shorter events, 177.7 us)
Async XLA Ops:
  43.3 15.4 %copy-start.11 = (f32[4,8,128]{2,1,0:T(8,128)S(1)}, f32[4,8,128]{2,1,0:T(8,128)}, u32[]{:S(2)}) copy-start(f32[4,8,128]{2,1,0:T(8,128)} %param.21) | copy-start | bytes 49156
  43.3 19.2 %copy-start.32 = (s32[2]{0:T(128)S(1)}, s32[2]{0:T(128)}, u32[]{:S(2)}) copy-start(s32[2]{0:T(128)} %constant.170) | copy-start | bytes 28
  43.3 19.3 %copy-start.33 = (s32[2]{0:T(128)S(1)}, s32[2]{0:T(128)}, u32[]{:S(2)}) copy-start(s32[2]{0:T(128)} %constant.173) | copy-start | bytes 28
  43.3 54.2 %all-to-all-start = ((bf16[64,32,512]{2,0,1:T(8,128)(2,1)}), bf16[64,32,512]{2,0,1:T(8,128)(2,1)S(1)}, u32[]{:S(2)}, u32[]{:S(2)}) async-start(bf16[64,32,512]{2,0,1:T(8,128)(2,1)} %copy.220), calls=%async_computation | async-start | bytes 4194304 | tf_op jit(solution)/shard_map/all_to_all | solution.py:87
  50.7 44.4 %slice-start = ((f32[4,8,128]{2,1,0:T(8,128)}), f32[3,8,128]{2,1,0:T(8,128)S(1)}, s32[]{:S(2)}) async-start(f32[4,8,128]{2,1,0:T(8,128)} %param.23), calls=%async_computation.2 | async-start | bytes 24576 | tf_op jit(solution)/shard_map/slice | solution.py:108
  50.7 44.5 %copy-start.9 = (f32[4,8,128]{2,1,0:T(8,128)S(1)}, f32[4,8,128]{2,1,0:T(8,128)}, u32[]{:S(2)}) copy-start(f32[4,8,128]{2,1,0:T(8,128)} %param.20) | copy-start | bytes 49156
  51.7 43.5 %collective-permute-start.2 = (f32[32,4,1,128]{3,0,2,1:T(8,128)S(1)}, f32[32,4,1,128]{3,0,2,1:T(8,128)S(1)}, u32[]{:S(2)}, u32[]{:S(2)}) collective-permute-start(f32[32,4,1,128]{3,0,2,1:T(8,128)S(1)} %get-tuple-element.215), channel_id=1, source_target_pairs={{0,4},{4,8},{8,12},{12,16},{16,20},{20,24},{24,28},{1,5},{5,9},{9,... | collective-permute-start | bytes 196616 | tf_op jit(solution)/shard_map/ppermute | solution.py:14
  53.8 43.6 %collective-permute-start = (f32[32,4,1,128]{3,0,2,1:T(8,128)}, f32[32,4,1,128]{3,0,2,1:T(8,128)S(1)}, u32[]{:S(2)}, u32[]{:S(2)}) collective-permute-start(f32[32,4,1,128]{3,0,2,1:T(8,128)} %get-tuple-element.214), channel_id=1, source_target_pairs={{4,0},{8,4},{12,8},{16,12},{20,16},{24,20},{28,24},{5,1},{9,5},{13... | collective-permute-start | bytes 196616 | tf_op jit(solution)/shard_map/ppermute | solution.py:17
  55.2 39.9 %collective-permute-start.4 = (f32[4,8,1]{2,1,0:T(8,128)S(1)}, f32[4,8,1]{2,1,0:T(8,128)S(1)}, u32[]{:S(2)}, u32[]{:S(2)}) collective-permute-start(f32[4,8,1]{2,1,0:T(8,128)S(1)} %slice.379), channel_id=1, source_target_pairs={{0,1},{1,2},{2,3},{4,5},{5,6},{6,7},{8,9},{9,10},{10,11},{12,13},{... | collective-permute-start | bytes 392 | tf_op jit(solution)/shard_map/ppermute | solution.py:25
  58.8 56.2 %collective-permute-start.1 = (f32[4,1,128]{2,1,0:T(1,128)S(1)}, f32[4,1,128]{2,1,0:T(1,128)S(1)}, u32[]{:S(2)}, u32[]{:S(2)}) collective-permute-start(f32[4,1,128]{2,1,0:T(1,128)S(1)} %slice.373), channel_id=1, source_target_pairs={{0,4},{4,8},{8,12},{12,16},{16,20},{20,24},{24,28},{1,5},{5,9},{9,... | collective-permute-start | bytes 6152 | tf_op jit(solution)/shard_map/ppermute | solution.py:25
  97.6 21.4 %all-to-all-start.1 = ((s32[1,32,512]{2,0,1:T(1,128)}), s32[1,32,512]{2,0,1:T(1,128)}, u32[]{:S(2)}, u32[]{:S(2)}) async-start(s32[1,32,512]{2,0,1:T(1,128)} %bitcast.344), calls=%async_computation.1 | async-start | bytes 131072 | tf_op jit(solution)/shard_map/all_to_all | solution.py:88
  107.6 7.4 %collective-permute-start.3 = (f32[32,4,10,1]{0,1,3,2:T(4,128)S(1)}, f32[32,4,10,1]{0,1,3,2:T(4,128)S(1)}, u32[]{:S(2)}, u32[]{:S(2)}) collective-permute-start(f32[32,4,10,1]{0,1,3,2:T(4,128)S(1)} %copy.230), channel_id=1, source_target_pairs={{1,0},{2,1},{3,2},{5,4},{6,5},{7,6},{9,8},{10,9},{11,10},{13,12},{... | collective-permute-start | bytes 15368 | tf_op jit(solution)/shard_map/ppermute | solution.py:17
  110.3 6.0 collective-permute-start.5
  119.0 55.4 %copy-start.4 = (f32[32,4,8,128]{3,0,2,1:T(8,128)S(1)}, f32[32,4,8,128]{3,0,2,1:T(8,128)}, u32[]{:S(2)}) copy-start(f32[32,4,8,128]{3,0,2,1:T(8,128)} %get-tuple-element.217) | copy-start | bytes 1572868
  119.0 55.5 %copy-start.5 = (f32[32,4,10,1]{3,0,2,1:T(8,128)S(1)}, f32[32,4,10,1]{3,0,2,1:T(8,128)}, u32[]{:S(2)}) copy-start(f32[32,4,10,1]{3,0,2,1:T(8,128)} %copy.231) | copy-start | bytes 15364
  119.0 55.5 %copy-start.7 = (f32[32,3,8,128]{3,0,2,1:T(8,128)S(1)}, f32[32,3,8,128]{3,0,2,1:T(8,128)}, u32[]{:S(2)}) copy-start(f32[32,3,8,128]{3,0,2,1:T(8,128)} %get-tuple-element.212) | copy-start | bytes 1179652
  119.0 55.5 %copy-start.12 = (f32[4,8,128]{2,1,0:T(8,128)S(1)}, f32[4,8,128]{2,1,0:T(8,128)}, u32[]{:S(2)}) copy-start(f32[4,8,128]{2,1,0:T(8,128)} %param.23) | copy-start | bytes 49156
  176.3 4.4 collective-permute-start.6
  177.6 3.9 collective-permute-start.7
  182.2 7.7 %collective-permute-start.8 = (f32[32,4,10,1]{0,1,3,2:T(4,128)S(1)}, f32[32,4,10,1]{0,1,3,2:T(4,128)S(1)}, u32[]{:S(2)}, u32[]{:S(2)}) collective-permute-start(f32[32,4,10,1]{0,1,3,2:T(4,128)S(1)} %copy.240), channel_id=1, source_target_pairs={{1,0},{2,1},{3,2},{5,4},{6,5},{7,6},{9,8},{10,9},{11,10},{13,12},{... | collective-permute-start | bytes 15368 | tf_op jit(solution)/shard_map/ppermute | solution.py:17
  183.8 6.4 collective-permute-start.9
  257.9 5.1 collective-permute-start.10
  259.2 3.9 collective-permute-start.11
  264.9 10.1 %collective-permute-start.12 = (f32[32,4,10,1]{0,1,3,2:T(4,128)S(1)}, f32[32,4,10,1]{0,1,3,2:T(4,128)S(1)}, u32[]{:S(2)}, u32[]{:S(2)}) collective-permute-start(f32[32,4,10,1]{0,1,3,2:T(4,128)S(1)} %copy.254), channel_id=1, source_target_pairs={{1,0},{2,1},{3,2},{5,4},{6,5},{7,6},{9,8},{10,9},{11,10},{13,12},{... | collective-permute-start | bytes 15368 | tf_op jit(solution)/shard_map/ppermute | solution.py:17
  266.5 8.9 %collective-permute-start.13 = (f32[32,4,10,1]{0,1,3,2:T(4,128)S(1)}, f32[32,4,10,1]{0,1,3,2:T(4,128)S(1)}, u32[]{:S(2)}, u32[]{:S(2)}) collective-permute-start(f32[32,4,10,1]{0,1,3,2:T(4,128)S(1)} %copy.256), channel_id=1, source_target_pairs={{0,1},{1,2},{2,3},{4,5},{5,6},{6,7},{8,9},{9,10},{10,11},{12,13},{... | collective-permute-start | bytes 15368 | tf_op jit(solution)/shard_map/ppermute | solution.py:14
  278.0 52.9 %copy-start.30 = (f32[1,32,32]{1,2,0:T(8,128)S(1)}, f32[1,32,32]{1,2,0:T(8,128)}, u32[]{:S(2)}) copy-start(f32[1,32,32]{1,2,0:T(8,128)} %custom-call.20) | copy-start | bytes 12292
  331.9 5.0 collective-permute-start.14
  333.2 3.9 collective-permute-start.15
  338.8 6.3 collective-permute-start.16
  340.4 6.0 collective-permute-start.17
  399.5 5.2 collective-permute-start.18
  400.8 3.9 collective-permute-start.19
  406.5 6.6 %collective-permute-start.20 = (f32[32,4,10,1]{0,1,3,2:T(4,128)S(1)}, f32[32,4,10,1]{0,1,3,2:T(4,128)S(1)}, u32[]{:S(2)}, u32[]{:S(2)}) collective-permute-start(f32[32,4,10,1]{0,1,3,2:T(4,128)S(1)} %copy.274), channel_id=1, source_target_pairs={{1,0},{2,1},{3,2},{5,4},{6,5},{7,6},{9,8},{10,9},{11,10},{13,12},{... | collective-permute-start | bytes 15368 | tf_op jit(solution)/shard_map/ppermute | solution.py:17
  408.1 6.0 collective-permute-start.21
  416.2 5.4 collective-permute-start.22
  417.5 4.2 collective-permute-start.23
  423.5 6.7 %collective-permute-start.24 = (f32[32,4,10,1]{0,1,3,2:T(4,128)S(1)}, f32[32,4,10,1]{0,1,3,2:T(4,128)S(1)}, u32[]{:S(2)}, u32[]{:S(2)}) collective-permute-start(f32[32,4,10,1]{0,1,3,2:T(4,128)S(1)} %copy.278), channel_id=1, source_target_pairs={{1,0},{2,1},{3,2},{5,4},{6,5},{7,6},{9,8},{10,9},{11,10},{13,12},{... | collective-permute-start | bytes 15368 | tf_op jit(solution)/shard_map/ppermute | solution.py:17
  425.1 6.0 collective-permute-start.25
  502.8 5.0 collective-permute-start.26
  504.1 3.9 collective-permute-start.27
  508.7 10.0 %collective-permute-start.28 = (f32[32,4,10,1]{0,1,3,2:T(4,128)S(1)}, f32[32,4,10,1]{0,1,3,2:T(4,128)S(1)}, u32[]{:S(2)}, u32[]{:S(2)}) collective-permute-start(f32[32,4,10,1]{0,1,3,2:T(4,128)S(1)} %copy.291), channel_id=1, source_target_pairs={{1,0},{2,1},{3,2},{5,4},{6,5},{7,6},{9,8},{10,9},{11,10},{13,12},{... | collective-permute-start | bytes 15368 | tf_op jit(solution)/shard_map/ppermute | solution.py:17
  510.3 8.8 %collective-permute-start.29 = (f32[32,4,10,1]{0,1,3,2:T(4,128)S(1)}, f32[32,4,10,1]{0,1,3,2:T(4,128)S(1)}, u32[]{:S(2)}, u32[]{:S(2)}) collective-permute-start(f32[32,4,10,1]{0,1,3,2:T(4,128)S(1)} %copy.293), channel_id=1, source_target_pairs={{0,1},{1,2},{2,3},{4,5},{5,6},{6,7},{8,9},{9,10},{10,11},{12,13},{... | collective-permute-start | bytes 15368 | tf_op jit(solution)/shard_map/ppermute | solution.py:14
  521.5 52.3 %copy-start.31 = (f32[1,32,32]{1,2,0:T(8,128)S(1)}, f32[1,32,32]{1,2,0:T(8,128)}, u32[]{:S(2)}) copy-start(f32[1,32,32]{1,2,0:T(8,128)} %custom-call.25) | copy-start | bytes 12292
  522.7 56.5 %copy-start.6 = (f32[32,4,8,128]{3,0,2,1:T(8,128)S(1)}, f32[32,4,8,128]{3,0,2,1:T(8,128)}, u32[]{:S(2)}) copy-start(f32[32,4,8,128]{3,0,2,1:T(8,128)} %convolution_add_fusion.4) | copy-start | bytes 1572868
  574.9 5.0 collective-permute-start.30
  576.2 3.9 collective-permute-start.31
  581.7 7.1 %collective-permute-start.32 = (f32[32,4,10,1]{0,1,3,2:T(4,128)S(1)}, f32[32,4,10,1]{0,1,3,2:T(4,128)S(1)}, u32[]{:S(2)}, u32[]{:S(2)}) collective-permute-start(f32[32,4,10,1]{0,1,3,2:T(4,128)S(1)} %copy.303), channel_id=1, source_target_pairs={{1,0},{2,1},{3,2},{5,4},{6,5},{7,6},{9,8},{10,9},{11,10},{13,12},{... | collective-permute-start | bytes 15368 | tf_op jit(solution)/shard_map/ppermute | solution.py:17
  583.3 6.0 collective-permute-start.33
  (25 other events, 150.4 us)
where the time goes:
time: 657 us; the launch traced here: 647 us
  blocking collectives  266 us (40%)
  local copies, waits for them, and re-layouts  107 us (16%)
  starting transfers between devices  104 us (16%)
  other arithmetic  95.1 us (14%)
  matrix products  68.5 us (10%)
    psum x4, blocking collectives, body(): lax.psum((gram(direction, image), gram(residual, image), gram(image, imag...  174 us
    psum x2, blocking collectives, body(): norm_gram = lax.psum(gram(residual, residual), ('gx', 'gy'))  91.3 us
    ppermute x16, starting transfers between devices, with_halo(): lax.ppermute(lax.slice_in_dim(block, block.shape[dim] - width, None, axis...  61.3 us
    dot_general x16, matrix products, add_block(): jnp.dot(piece_values, one_hot, preferred_element_type=jnp.float32)  42.7 us
    unnamed x79, local copies, waits for them, and re-layouts  40.2 us
    another operation x30, other arithmetic, spd_solve(): factor = jnp.linalg.cholesky(matrix)  36.1 us
    another operation x20, other arithmetic, spd_solve(): return jax.scipy.linalg.cho_solve((factor, True), right)  32.2 us
    scatter x1, local copies, waits for them, and re-layouts, body(): jnp.zeros((currents.shape[0], slots_all), jnp.bfloat16).at[:, slot_index]  23.7 us
  transfers between devices with their start and end apart: 36, of which 11 were waited for; matrix products, arithmetic and copies ran while one was open for 10% of the time, Pallas kernels for 0%

commit v1 on v0

--- a/solution.py
+++ b/solution.py
@@ -118,7 +118,9 @@
         iterate = voltage
         residual = rhs - apply_grid(iterate)
         direction = residual
-        norm_gram = lax.psum(gram(residual, residual), ("gx", "gy"))
+        norm_gram = gram(residual, residual)
+        for m in ("gy", "gx"):
+            norm_gram = lax.psum(norm_gram, axis_name=m)
         for sweep in range(ITERS):
             image = apply_grid(direction)
             curve_gram, cross_gram, image_gram = lax.psum(

time: 657 us -> 727 us (1.11)
  blocking collectives: 266 us -> 337 us
    psum x4 -> x6, blocking collectives: 174 us -> 253 us  [body(): lax.psum((gram(direction, image), gram(residual, image), gram(image, imag...]
    psum x2 -> x4, blocking collectives: 91.3 us -> 84 us  [body(): norm_gram = lax.psum(norm_gram, axis_name=m)]
  transfers between devices with their start and end apart: 36 -> 36, of which waited for: 11 -> 9; matrix products, arithmetic and copies ran while one was open for 10% -> 10% of each run, Pallas kernels for 0% -> 0%
where the time goes in v1:
time: 727 us; the launch traced here: 717 us
  blocking collectives  337 us (46%)
  local copies, waits for them, and re-layouts  107 us (15%)
  starting transfers between devices  104 us (14%)
  other arithmetic  96 us (13%)
  matrix products  68.3 us (9%)
    psum x6, blocking collectives, body(): lax.psum((gram(direction, image), gram(residual, image), gram(image, imag...  253 us
    psum x4, blocking collectives, body(): norm_gram = lax.psum(norm_gram, axis_name=m)  84 us
    ppermute x16, starting transfers between devices, with_halo(): lax.ppermute(lax.slice_in_dim(block, block.shape[dim] - width, None, axis...  61 us
    dot_general x16, matrix products, add_block(): jnp.dot(piece_values, one_hot, preferred_element_type=jnp.float32)  42.6 us
    unnamed x79, local copies, waits for them, and re-layouts  39.6 us
    another operation x30, other arithmetic, spd_solve(): factor = jnp.linalg.cholesky(matrix)  36.1 us
    another operation x20, other arithmetic, spd_solve(): return jax.scipy.linalg.cho_solve((factor, True), right)  32.1 us
    scatter x1, local copies, waits for them, and re-layouts, body(): jnp.zeros((currents.shape[0], slots_all), jnp.bfloat16).at[:, slot_index]  23.6 us
  transfers between devices with their start and end apart: 36, of which 9 were waited for; matrix products, arithmetic and copies ran while one was open for 10% of the time, Pallas kernels for 0%

profile of v1, /device:TPU:0, one launch (start us, length us, event | category | flops | bytes accessed | tf_op | source)
XLA Modules:
  0.0 717.0 jit_solution(2779249280779818831)
XLA Ops:
  1.6 9.5 %reduce-window.6 = s32[32,64,128]{2,1,0:T(8,128)S(1)} reduce-window(s32[32,64,128]{2,1,0:T(8,128)S(1)} %fusion.11, s32[]{:T(128)} %constant.128.clone.1), window={size=1x1x128 pad=0_0x0_0x127_0}, to_apply=%region_0.0 | reduce-window | flops 33292288 | bytes 2097156 | tf_op jit(solution)/shard_map/reduce-window
  14.9 23.6 %scatter_custom_fusion = bf16[64,16384]{0,1:T(8,128)(2,1)} fusion(s32[8192]{0:T(1024)S(1)} %bitcast.343, bf16[8192,64]{1,0:T(8,128)(2,1)S(1)} %copy.219, bf16[]{:T(256)} %constant.130.clone.1), kind=kCustom, calls=%fused_computation.13 | custom fusion | bytes 2097154 | tf_op jit(solution)/shard_map/scatter | solution.py:84
  38.5 4.8 copy.220
  43.3 7.3 %all-to-all-start = ((bf16[64,32,512]{2,0,1:T(8,128)(2,1)}), bf16[64,32,512]{2,0,1:T(8,128)(2,1)S(1)}, u32[]{:S(2)}, u32[]{:S(2)}) async-start(bf16[64,32,512]{2,0,1:T(8,128)(2,1)} %copy.220), calls=%async_computation | async-start | bytes 4194304 | tf_op jit(solution)/shard_map/all_to_all | solution.py:87
  55.2 3.5 collective-permute-start.4
  58.8 3.7 collective-permute-start.1
  62.9 31.2 %scatter_custom_fusion.1 = s32[16384]{0:T(1024)} fusion(s32[8192]{0:T(1024)S(1)} %broadcast_select_fusion, s32[8192]{0:T(1024)} %param.26, s32[]{:T(128)} %constant.128.clone.1), kind=kCustom, calls=%fused_computation.270 | custom fusion | bytes 66048
  97.6 7.3 %all-to-all-start.1 = ((s32[1,32,512]{2,0,1:T(1,128)}), s32[1,32,512]{2,0,1:T(1,128)}, u32[]{:S(2)}, u32[]{:S(2)}) async-start(s32[1,32,512]{2,0,1:T(1,128)} %bitcast.344), calls=%async_computation.1 | async-start | bytes 131072 | tf_op jit(solution)/shard_map/all_to_all | solution.py:88
  110.2 4.7 collective-permute-start.5
  119.0 53.6 %while.16 = (s32[]{:T(128)}, f32[64,1024]{1,0:T(8,128)}, bf16[64,16384]{1,0:T(8,128)(2,1)}, s32[1,16384]{1,0:T(1,128)}, s32[]{:T(128)}, /*index=5*/s32[]{:T(128)}, s32[]{:T(128)}, s32[]{:T(128)}) while((s32[]{:T(128)}, f32[64,1024]{1,0:T(8,128)}, bf16[64,16384]{1,0:T(8,128)(2,1)}, s32[1,16384]{1,0:T(1,128)}, s32[]{:T(128)}, ...), condition=%wide.region_6.7_spmd.clone, body=%wide.region_5.6_spmd.clone.sunk | while | flops 135397376 | bytes 667797 | solution.py:100
  163.2 2.7 fusion.346
  169.9 2.7 fusion.346
  178.1 3.0 collective-permute-start.7
  181.2 19.7 %psum.119 = f32[32,32]{0,1:T(8,128)S(1)} all-reduce(f32[32,32]{0,1:T(8,128)S(1)} %convolution_bitcast_fusion.18), channel_id=1, replica_groups=mesh['gx'=8,'gy'=4] {'gy'}, use_global_device_ids=true, to_apply=%region_10.12 | all-reduce | flops 1024 | bytes 8192 | tf_op jit(solution)/shard_map/psum | solution.py:123
  200.9 22.3 %psum.120 = f32[32,32]{0,1:T(8,128)S(1)} all-reduce(f32[32,32]{0,1:T(8,128)S(1)} %psum.119), channel_id=1, replica_groups=mesh['gx'=8,'gy'=4] {'gx'}, use_global_device_ids=true, to_apply=%region_11.13 | all-reduce | flops 1024 | bytes 8192 | tf_op jit(solution)/shard_map/psum | solution.py:123
  223.3 2.9 cholesky.175
  229.7 4.5 collective-permute-start.9
  241.3 37.9 %all-reduce.21 = (f32[32,32]{0,1:T(8,128)S(1)}, f32[32,32]{1,0:T(8,128)S(1)}) all-reduce(f32[32,32]{0,1:T(8,128)S(1)} %convolution_bitcast_fusion.19, f32[32,32]{1,0:T(8,128)S(1)} %convolution_bitcast_fusion.17), channel_id=1, replica_groups=mesh['gx'=8,'gy'=4] {'gx','gy'}, use_global_device_ids=true, to_apply=%region_7.8 | all-reduce | flops 2048 | bytes 16384 | tf_op jit(solution)/shard_map/psum | solution.py:126
  279.3 2.9 cholesky.164
  290.7 2.9 cholesky.197
  294.9 3.0 collective-permute-start.11
  302.1 4.8 collective-permute-start.13
  307.5 3.1 custom-call.20
  314.7 43.8 %all-reduce.20 = (f32[32,32]{0,1:T(8,128)S(1)}, f32[32,32]{1,0:T(8,128)S(1)}, f32[32,32]{1,0:T(8,128)S(1)}) all-reduce(f32[32,32]{0,1:T(8,128)S(1)} %convolution_bitcast_fusion.15, f32[32,32]{1,0:T(8,128)S(1)} %convolution_bitcast_fusion.13, f32[32,32]{1,0:T(8,128)S(1)} %convolution_bitcast_fusion.14), channel_id=1, replica_groups=mesh['gx'=8,'gy'=4] {'gx','gy'}, use_global_device_ids=true, to_apply=%region_13.16 | all-reduce | flops 3072 | bytes 24576 | tf_op jit(solution)/shard_map/psum | solution.py:126
  358.7 2.9 cholesky.186
  369.3 3.0 collective-permute-start.15
  376.5 4.5 collective-permute-start.17
  383.9 43.8 %psum.125 = f32[32,32]{0,1:T(8,128)S(1)} all-reduce(f32[32,32]{0,1:T(8,128)S(1)} %convolution_bitcast_fusion.11), channel_id=1, replica_groups=mesh['gx'=8,'gy'=4] {'gx','gy'}, use_global_device_ids=true, to_apply=%region_16.19 | all-reduce | flops 1024 | bytes 8192 | tf_op jit(solution)/shard_map/psum | solution.py:126
  427.7 2.9 cholesky.208
  436.8 3.0 collective-permute-start.19
  444.3 5.0 collective-permute-start.21
  455.1 3.3 collective-permute-start.23
  458.4 17.4 %psum.127 = f32[32,32]{0,1:T(8,128)S(1)} all-reduce(f32[32,32]{0,1:T(8,128)S(1)} %convolution_bitcast_fusion.8), channel_id=1, replica_groups=mesh['gx'=8,'gy'=4] {'gy'}, use_global_device_ids=true, to_apply=%region_18.21 | all-reduce | flops 1024 | bytes 8192 | tf_op jit(solution)/shard_map/psum | solution.py:123
  475.9 24.6 %psum.128 = f32[32,32]{0,1:T(8,128)S(1)} all-reduce(f32[32,32]{0,1:T(8,128)S(1)} %psum.127), channel_id=1, replica_groups=mesh['gx'=8,'gy'=4] {'gx'}, use_global_device_ids=true, to_apply=%region_19.22 | all-reduce | flops 1024 | bytes 8192 | tf_op jit(solution)/shard_map/psum | solution.py:123
  500.5 2.9 cholesky.230
  506.4 4.5 collective-permute-start.25
  517.6 39.0 %all-reduce.19 = (f32[32,32]{0,1:T(8,128)S(1)}, f32[32,32]{1,0:T(8,128)S(1)}) all-reduce(f32[32,32]{0,1:T(8,128)S(1)} %convolution_bitcast_fusion.9, f32[32,32]{1,0:T(8,128)S(1)} %convolution_bitcast_fusion.7), channel_id=1, replica_groups=mesh['gx'=8,'gy'=4] {'gx','gy'}, use_global_device_ids=true, to_apply=%region_17.20 | all-reduce | flops 2048 | bytes 16384 | tf_op jit(solution)/shard_map/psum | solution.py:126
  556.6 2.9 cholesky.219
  568.5 2.9 cholesky.252
  572.8 3.0 collective-permute-start.27
  578.9 4.7 collective-permute-start.29
  584.3 3.1 custom-call.25
  591.3 44.4 %all-reduce.18 = (f32[32,32]{0,1:T(8,128)S(1)}, f32[32,32]{1,0:T(8,128)S(1)}, f32[32,32]{1,0:T(8,128)S(1)}) all-reduce(f32[32,32]{0,1:T(8,128)S(1)} %convolution_bitcast_fusion.5, f32[32,32]{1,0:T(8,128)S(1)} %convolution_bitcast_fusion.3, f32[32,32]{1,0:T(8,128)S(1)} %convolution_bitcast_fusion.4), channel_id=1, replica_groups=mesh['gx'=8,'gy'=4] {'gx','gy'}, use_global_device_ids=true, to_apply=%region_21.24 | all-reduce | flops 3072 | bytes 24576 | tf_op jit(solution)/shard_map/psum | solution.py:126
  635.9 2.9 cholesky.241
  646.5 3.0 collective-permute-start.31
  653.7 4.5 collective-permute-start.33
  662.4 43.8 %psum.133 = f32[32,32]{0,1:T(8,128)S(1)} all-reduce(f32[32,32]{0,1:T(8,128)S(1)} %convolution_bitcast_fusion.1), channel_id=1, replica_groups=mesh['gx'=8,'gy'=4] {'gx','gy'}, use_global_device_ids=true, to_apply=%region_24.27 | all-reduce | flops 1024 | bytes 8192 | tf_op jit(solution)/shard_map/psum | solution.py:126
  706.2 2.9 cholesky.263
  (378 shorter events, 187.3 us)
Async XLA Ops:
  43.3 15.4 %copy-start.11 = (f32[4,8,128]{2,1,0:T(8,128)S(1)}, f32[4,8,128]{2,1,0:T(8,128)}, u32[]{:S(2)}) copy-start(f32[4,8,128]{2,1,0:T(8,128)} %param.21) | copy-start | bytes 49156
  43.3 19.2 %copy-start.32 = (s32[2]{0:T(128)S(1)}, s32[2]{0:T(128)}, u32[]{:S(2)}) copy-start(s32[2]{0:T(128)} %constant.170) | copy-start | bytes 28
  43.3 19.3 %copy-start.33 = (s32[2]{0:T(128)S(1)}, s32[2]{0:T(128)}, u32[]{:S(2)}) copy-start(s32[2]{0:T(128)} %constant.173) | copy-start | bytes 28
  43.3 54.2 %all-to-all-start = ((bf16[64,32,512]{2,0,1:T(8,128)(2,1)}), bf16[64,32,512]{2,0,1:T(8,128)(2,1)S(1)}, u32[]{:S(2)}, u32[]{:S(2)}) async-start(bf16[64,32,512]{2,0,1:T(8,128)(2,1)} %copy.220), calls=%async_computation | async-start | bytes 4194304 | tf_op jit(solution)/shard_map/all_to_all | solution.py:87
  50.7 44.4 %slice-start = ((f32[4,8,128]{2,1,0:T(8,128)}), f32[3,8,128]{2,1,0:T(8,128)S(1)}, s32[]{:S(2)}) async-start(f32[4,8,128]{2,1,0:T(8,128)} %param.23), calls=%async_computation.2 | async-start | bytes 24576 | tf_op jit(solution)/shard_map/slice | solution.py:108
  50.7 44.5 %copy-start.9 = (f32[4,8,128]{2,1,0:T(8,128)S(1)}, f32[4,8,128]{2,1,0:T(8,128)}, u32[]{:S(2)}) copy-start(f32[4,8,128]{2,1,0:T(8,128)} %param.20) | copy-start | bytes 49156
  51.7 43.5 %collective-permute-start.2 = (f32[32,4,1,128]{3,0,2,1:T(8,128)S(1)}, f32[32,4,1,128]{3,0,2,1:T(8,128)S(1)}, u32[]{:S(2)}, u32[]{:S(2)}) collective-permute-start(f32[32,4,1,128]{3,0,2,1:T(8,128)S(1)} %get-tuple-element.213), channel_id=1, source_target_pairs={{0,4},{4,8},{8,12},{12,16},{16,20},{20,24},{24,28},{1,5},{5,9},{9,... | collective-permute-start | bytes 196616 | tf_op jit(solution)/shard_map/ppermute | solution.py:14
  53.8 43.6 %collective-permute-start = (f32[32,4,1,128]{3,0,2,1:T(8,128)}, f32[32,4,1,128]{3,0,2,1:T(8,128)S(1)}, u32[]{:S(2)}, u32[]{:S(2)}) collective-permute-start(f32[32,4,1,128]{3,0,2,1:T(8,128)} %get-tuple-element.212), channel_id=1, source_target_pairs={{4,0},{8,4},{12,8},{16,12},{20,16},{24,20},{28,24},{5,1},{9,5},{13... | collective-permute-start | bytes 196616 | tf_op jit(solution)/shard_map/ppermute | solution.py:17
  55.2 39.9 %collective-permute-start.4 = (f32[4,8,1]{2,1,0:T(8,128)S(1)}, f32[4,8,1]{2,1,0:T(8,128)S(1)}, u32[]{:S(2)}, u32[]{:S(2)}) collective-permute-start(f32[4,8,1]{2,1,0:T(8,128)S(1)} %slice.379), channel_id=1, source_target_pairs={{0,1},{1,2},{2,3},{4,5},{5,6},{6,7},{8,9},{9,10},{10,11},{12,13},{... | collective-permute-start | bytes 392 | tf_op jit(solution)/shard_map/ppermute | solution.py:25
  58.8 56.2 %collective-permute-start.1 = (f32[4,1,128]{2,1,0:T(1,128)S(1)}, f32[4,1,128]{2,1,0:T(1,128)S(1)}, u32[]{:S(2)}, u32[]{:S(2)}) collective-permute-start(f32[4,1,128]{2,1,0:T(1,128)S(1)} %slice.373), channel_id=1, source_target_pairs={{0,4},{4,8},{8,12},{12,16},{16,20},{20,24},{24,28},{1,5},{5,9},{9,... | collective-permute-start | bytes 6152 | tf_op jit(solution)/shard_map/ppermute | solution.py:25
  97.6 21.4 %all-to-all-start.1 = ((s32[1,32,512]{2,0,1:T(1,128)}), s32[1,32,512]{2,0,1:T(1,128)}, u32[]{:S(2)}, u32[]{:S(2)}) async-start(s32[1,32,512]{2,0,1:T(1,128)} %bitcast.344), calls=%async_computation.1 | async-start | bytes 131072 | tf_op jit(solution)/shard_map/all_to_all | solution.py:88
  107.5 7.4 %collective-permute-start.3 = (f32[32,4,10,1]{0,1,3,2:T(4,128)S(1)}, f32[32,4,10,1]{0,1,3,2:T(4,128)S(1)}, u32[]{:S(2)}, u32[]{:S(2)}) collective-permute-start(f32[32,4,10,1]{0,1,3,2:T(4,128)S(1)} %copy.230), channel_id=1, source_target_pairs={{1,0},{2,1},{3,2},{5,4},{6,5},{7,6},{9,8},{10,9},{11,10},{13,12},{... | collective-permute-start | bytes 15368 | tf_op jit(solution)/shard_map/ppermute | solution.py:17
  110.2 6.0 collective-permute-start.5
  119.0 55.3 %copy-start.4 = (f32[32,4,8,128]{3,0,2,1:T(8,128)S(1)}, f32[32,4,8,128]{3,0,2,1:T(8,128)}, u32[]{:S(2)}) copy-start(f32[32,4,8,128]{3,0,2,1:T(8,128)} %get-tuple-element.215) | copy-start | bytes 1572868
  119.0 55.3 %copy-start.5 = (f32[32,4,10,1]{3,0,2,1:T(8,128)S(1)}, f32[32,4,10,1]{3,0,2,1:T(8,128)}, u32[]{:S(2)}) copy-start(f32[32,4,10,1]{3,0,2,1:T(8,128)} %copy.231) | copy-start | bytes 15364
  119.0 55.4 %copy-start.7 = (f32[32,3,8,128]{3,0,2,1:T(8,128)S(1)}, f32[32,3,8,128]{3,0,2,1:T(8,128)}, u32[]{:S(2)}) copy-start(f32[32,3,8,128]{3,0,2,1:T(8,128)} %get-tuple-element.210) | copy-start | bytes 1179652
  119.0 55.4 %copy-start.12 = (f32[4,8,128]{2,1,0:T(8,128)S(1)}, f32[4,8,128]{2,1,0:T(8,128)}, u32[]{:S(2)}) copy-start(f32[4,8,128]{2,1,0:T(8,128)} %param.23) | copy-start | bytes 49156
  176.8 50.1 %collective-permute-start.6 = (f32[32,4,1,128]{3,0,2,1:T(8,128)S(1)}, f32[32,4,1,128]{3,0,2,1:T(8,128)S(1)}, u32[]{:S(2)}, u32[]{:S(2)}) collective-permute-start(f32[32,4,1,128]{3,0,2,1:T(8,128)S(1)} %get-tuple-element.209), channel_id=1, source_target_pairs={{4,0},{8,4},{12,8},{16,12},{20,16},{24,20},{28,24},{5,1},{9,5},{13... | collective-permute-start | bytes 196616 | tf_op jit(solution)/shard_map/ppermute | solution.py:17
  178.1 48.8 %collective-permute-start.7 = (f32[32,4,1,128]{3,0,2,1:T(8,128)S(1)}, f32[32,4,1,128]{3,0,2,1:T(8,128)S(1)}, u32[]{:S(2)}, u32[]{:S(2)}) collective-permute-start(f32[32,4,1,128]{3,0,2,1:T(8,128)S(1)} %get-tuple-element.208), channel_id=1, source_target_pairs={{0,4},{4,8},{8,12},{12,16},{16,20},{20,24},{24,28},{1,5},{5,9},{9,... | collective-permute-start | bytes 196616 | tf_op jit(solution)/shard_map/ppermute | solution.py:14
  228.1 9.9 %collective-permute-start.8 = (f32[32,4,10,1]{0,1,3,2:T(4,128)S(1)}, f32[32,4,10,1]{0,1,3,2:T(4,128)S(1)}, u32[]{:S(2)}, u32[]{:S(2)}) collective-permute-start(f32[32,4,10,1]{0,1,3,2:T(4,128)S(1)} %copy.240), channel_id=1, source_target_pairs={{1,0},{2,1},{3,2},{5,4},{6,5},{7,6},{9,8},{10,9},{11,10},{13,12},{... | collective-permute-start | bytes 15368 | tf_op jit(solution)/shard_map/ppermute | solution.py:17
  229.7 8.7 %collective-permute-start.9 = (f32[32,4,10,1]{0,1,3,2:T(4,128)S(1)}, f32[32,4,10,1]{0,1,3,2:T(4,128)S(1)}, u32[]{:S(2)}, u32[]{:S(2)}) collective-permute-start(f32[32,4,10,1]{0,1,3,2:T(4,128)S(1)} %copy.242), channel_id=1, source_target_pairs={{0,1},{1,2},{2,3},{4,5},{5,6},{6,7},{8,9},{9,10},{10,11},{12,13},{... | collective-permute-start | bytes 15368 | tf_op jit(solution)/shard_map/ppermute | solution.py:14
  293.6 5.0 collective-permute-start.10
  294.9 3.9 collective-permute-start.11
  300.5 10.1 %collective-permute-start.12 = (f32[32,4,10,1]{0,1,3,2:T(4,128)S(1)}, f32[32,4,10,1]{0,1,3,2:T(4,128)S(1)}, u32[]{:S(2)}, u32[]{:S(2)}) collective-permute-start(f32[32,4,10,1]{0,1,3,2:T(4,128)S(1)} %copy.254), channel_id=1, source_target_pairs={{1,0},{2,1},{3,2},{5,4},{6,5},{7,6},{9,8},{10,9},{11,10},{13,12},{... | collective-permute-start | bytes 15368 | tf_op jit(solution)/shard_map/ppermute | solution.py:17
  302.1 8.8 %collective-permute-start.13 = (f32[32,4,10,1]{0,1,3,2:T(4,128)S(1)}, f32[32,4,10,1]{0,1,3,2:T(4,128)S(1)}, u32[]{:S(2)}, u32[]{:S(2)}) collective-permute-start(f32[32,4,10,1]{0,1,3,2:T(4,128)S(1)} %copy.256), channel_id=1, source_target_pairs={{0,1},{1,2},{2,3},{4,5},{5,6},{6,7},{8,9},{9,10},{10,11},{12,13},{... | collective-permute-start | bytes 15368 | tf_op jit(solution)/shard_map/ppermute | solution.py:14
  313.6 53.4 %copy-start.30 = (f32[1,32,32]{1,2,0:T(8,128)S(1)}, f32[1,32,32]{1,2,0:T(8,128)}, u32[]{:S(2)}) copy-start(f32[1,32,32]{1,2,0:T(8,128)} %custom-call.20) | copy-start | bytes 12292
  368.0 5.0 collective-permute-start.14
  369.3 3.9 collective-permute-start.15
  374.9 6.3 collective-permute-start.16
  376.5 6.0 collective-permute-start.17
  435.5 5.3 collective-permute-start.18
  436.8 4.0 collective-permute-start.19
  442.7 6.6 collective-permute-start.20
  444.3 6.0 collective-permute-start.21
  453.8 50.4 %collective-permute-start.22 = (f32[32,4,1,128]{3,0,2,1:T(8,128)S(1)}, f32[32,4,1,128]{3,0,2,1:T(8,128)S(1)}, u32[]{:S(2)}, u32[]{:S(2)}) collective-permute-start(f32[32,4,1,128]{3,0,2,1:T(8,128)S(1)} %get-tuple-element.193), channel_id=1, source_target_pairs={{4,0},{8,4},{12,8},{16,12},{20,16},{24,20},{28,24},{5,1},{9,5},{13... | collective-permute-start | bytes 196616 | tf_op jit(solution)/shard_map/ppermute | solution.py:17
  455.1 49.1 %collective-permute-start.23 = (f32[32,4,1,128]{3,0,2,1:T(8,128)S(1)}, f32[32,4,1,128]{3,0,2,1:T(8,128)S(1)}, u32[]{:S(2)}, u32[]{:S(2)}) collective-permute-start(f32[32,4,1,128]{3,0,2,1:T(8,128)S(1)} %get-tuple-element.192), channel_id=1, source_target_pairs={{0,4},{4,8},{8,12},{12,16},{16,20},{20,24},{24,28},{1,5},{5,9},{9,... | collective-permute-start | bytes 196616 | tf_op jit(solution)/shard_map/ppermute | solution.py:14
  504.8 9.3 %collective-permute-start.24 = (f32[32,4,10,1]{0,1,3,2:T(4,128)S(1)}, f32[32,4,10,1]{0,1,3,2:T(4,128)S(1)}, u32[]{:S(2)}, u32[]{:S(2)}) collective-permute-start(f32[32,4,10,1]{0,1,3,2:T(4,128)S(1)} %copy.278), channel_id=1, source_target_pairs={{1,0},{2,1},{3,2},{5,4},{6,5},{7,6},{9,8},{10,9},{11,10},{13,12},{... | collective-permute-start | bytes 15368 | tf_op jit(solution)/shard_map/ppermute | solution.py:17
  506.4 8.0 %collective-permute-start.25 = (f32[32,4,10,1]{0,1,3,2:T(4,128)S(1)}, f32[32,4,10,1]{0,1,3,2:T(4,128)S(1)}, u32[]{:S(2)}, u32[]{:S(2)}) collective-permute-start(f32[32,4,10,1]{0,1,3,2:T(4,128)S(1)} %copy.280), channel_id=1, source_target_pairs={{0,1},{1,2},{2,3},{4,5},{5,6},{6,7},{8,9},{9,10},{10,11},{12,13},{... | collective-permute-start | bytes 15368 | tf_op jit(solution)/shard_map/ppermute | solution.py:14
  571.5 5.0 collective-permute-start.26
  572.8 3.9 collective-permute-start.27
  577.3 10.0 %collective-permute-start.28 = (f32[32,4,10,1]{0,1,3,2:T(4,128)S(1)}, f32[32,4,10,1]{0,1,3,2:T(4,128)S(1)}, u32[]{:S(2)}, u32[]{:S(2)}) collective-permute-start(f32[32,4,10,1]{0,1,3,2:T(4,128)S(1)} %copy.291), channel_id=1, source_target_pairs={{1,0},{2,1},{3,2},{5,4},{6,5},{7,6},{9,8},{10,9},{11,10},{13,12},{... | collective-permute-start | bytes 15368 | tf_op jit(solution)/shard_map/ppermute | solution.py:17
  578.9 8.7 %collective-permute-start.29 = (f32[32,4,10,1]{0,1,3,2:T(4,128)S(1)}, f32[32,4,10,1]{0,1,3,2:T(4,128)S(1)}, u32[]{:S(2)}, u32[]{:S(2)}) collective-permute-start(f32[32,4,10,1]{0,1,3,2:T(4,128)S(1)} %copy.293), channel_id=1, source_target_pairs={{0,1},{1,2},{2,3},{4,5},{5,6},{6,7},{8,9},{9,10},{10,11},{12,13},{... | collective-permute-start | bytes 15368 | tf_op jit(solution)/shard_map/ppermute | solution.py:14
  590.2 54.0 %copy-start.31 = (f32[1,32,32]{1,2,0:T(8,128)S(1)}, f32[1,32,32]{1,2,0:T(8,128)}, u32[]{:S(2)}) copy-start(f32[1,32,32]{1,2,0:T(8,128)} %custom-call.25) | copy-start | bytes 12292
  591.3 58.2 %copy-start.6 = (f32[32,4,8,128]{3,0,2,1:T(8,128)S(1)}, f32[32,4,8,128]{3,0,2,1:T(8,128)}, u32[]{:S(2)}) copy-start(f32[32,4,8,128]{3,0,2,1:T(8,128)} %convolution_add_fusion.4) | copy-start | bytes 1572868
  645.2 5.0 collective-permute-start.30
  646.5 3.9 collective-permute-start.31
  652.1 7.1 collective-permute-start.32
  653.7 6.0 collective-permute-start.33
  (25 other events, 145.8 us)
